TPU v7x, 256 devices: a whole 4x4x8 slice. The times are simulated.
256 devices in a mesh: grp: 4 (over y), slab: 64 (over z, x, core).
Axes of the slice: x: 4, y: 4, z: 8, core: 2. Of those that a mesh axis runs over, the one named last changes fastest.
Arguments:
- velocity: float32 [16, 3, 4, 131072], P(None, None, 'grp', 'slab'), may hold values from -6 to 6
- old_basis: bfloat16 [64, 3, 4, 131072], P(None, None, None, 'slab'), may hold values from -6 to 6
- singular_values: float32 [64], replicated, may hold values from 0.7 to 1.4
- thickness: int32 [4, 64], P('grp', 'slab'), may hold values from 1 to 4, as said below
Outputs:
- gram_matrix: float32 [80, 80], replicated
- new_basis: bfloat16 [64, 3, 4, 131072], P(None, None, None, 'slab')
- offsets: int32 [4, 64], P('grp', 'slab')
Inputs may be any that keep to these rules, and one draw needn't show every extreme that they name: `thickness`: the entry at row-major position p differs from 1 + (p * 3) // 256 by at most one. The first entry is 1 and the last is 4.
All inputs are finite; a program needn't handle non-finite values.
Results may differ from a plain program's by a relative error of at most 0.0004.
The roundings to bfloat16 on the way count: a program that leaves them out, or rounds other values in their place, can miss the bound.
Values may be sent and summed in bfloat16 or wider, within the bound.
No kernel may reach another device: no remote copies, remote signals or barrier semaphores. Data moves between devices by JAX's collectives and lax.ppermute only.
A program may use at most 64 MiB of HBM per device.

v0:
```python
import jax
import jax.numpy as jnp
from jax import lax
from jax.experimental import pallas as pl
from jax.experimental.pallas import tpu as pltpu
from jax.sharding import Mesh
from jax.sharding import PartitionSpec as P


PLANE = 512
SLAB = ("slab_0", "slab_1", "slab_2")

R = 64
S = 16
N = R + S
G = 4
COLS = 6144
J = 48
ROWS = 192
PITCH = ROWS + 1
WIDE = (R + 1) * PITCH + 7
HIGHEST = lax.Precision.HIGHEST
MIB = 2**20


def vmem(n=1):
    return [pl.BlockSpec(memory_space=pltpu.VMEM) for _ in range(n)]


def smem():
    return pl.BlockSpec(memory_space=pltpu.SMEM)


def hbm(n=1):
    return [pl.BlockSpec(memory_space=pltpu.HBM) for _ in range(n)]


def near(x):
    return pltpu.with_memory_space_constraint(x, pltpu.VMEM)


def far(x):
    return pltpu.with_memory_space_constraint(x, pltpu.HBM)


def live_tile(t, thick, rows):
    return jnp.full((rows, 128), jnp.where(t // 4 < thick, 1, 0), jnp.int32) > 0


def snapshots_body(thick_ref, vel_hbm, snap_ref, vel_ref, sem):
    get = pltpu.make_async_copy(vel_hbm, vel_ref, sem)
    get.start()
    get.wait()
    thick = thick_ref[0, 0]
    for j in range(J):
        rows = vel_ref[pl.ds(j, S, stride=J), :]
        rows = jnp.where(live_tile(j % 16, thick, S), rows, 0.0)
        snap_ref[:, pl.ds(j * 128, 128)] = rows.astype(jnp.bfloat16)


def snapshots(thickness, velocity):
    return pl.pallas_call(
        snapshots_body,
        out_shape=pltpu.VMEM((S, COLS), jnp.bfloat16),
        in_specs=[smem()] + hbm(),
        out_specs=vmem()[0],
        scratch_shapes=[pltpu.VMEM((S * J, 128), jnp.float32), pltpu.SemaphoreType.DMA(())],
        compiler_params=pltpu.CompilerParams(vmem_limit_bytes=2 * MIB),
        cost_estimate=pl.CostEstimate(flops=2 * 10**9, transcendentals=0, bytes_accessed=10**6),
        name="snapshots",
    )(thickness, far(velocity.reshape(S * J, 128)))


def gram_body(thick_ref, basis_ref, snap_ref, wide_ref, keep_ref, send_ref, stack_ref):
    g = lax.axis_index("grp")
    core = lax.axis_index("slab_2")
    place = ((g * 8 + lax.axis_index("slab_0")) * 4 + lax.axis_index("slab_1")) * 2 + core
    thick = thick_ref[0, 0]

    def widen(r, _):
        wide_ref[pl.ds(r * PITCH, ROWS), :] = basis_ref[r].astype(jnp.float32)
        return 0

    lax.fori_loop(0, R, widen, 0, unroll=4)
    for j in range(J):
        rows = wide_ref[pl.ds(j * G + g, R, stride=PITCH), :]
        rows = jnp.where(live_tile(j % 16, thick, R), rows, 0.0)
        stack_ref[0:R, pl.ds(j * 128, 128)] = rows.astype(jnp.bfloat16)
    stack_ref[R:N, :] = snap_ref[...]
    stack_ref[N:, :] = jnp.zeros((128 - N, COLS), jnp.bfloat16)
    stacked = stack_ref[...]
    gram = lax.dot_general(
        stacked, stacked, (((1,), (1,)), ((), ())), preferred_element_type=jnp.float32
    )
    lane = lax.broadcasted_iota(jnp.int32, (16, 128), 1)
    row = lax.broadcasted_iota(jnp.int32, (16, 128), 0)
    thick_block = jnp.where(row * 16 + lane == place, thick.astype(jnp.float32), 0.0)
    upper = jnp.where(lane < 80, gram[0:16], pltpu.roll(gram[32:48], 48, 1))
    last = jnp.where(lane < 112, pltpu.roll(gram[48:64], 32, 1), pltpu.roll(gram[64:80], 48, 1))
    lower = jnp.where(lane < 16, thick_block, jnp.where(lane < 80, gram[16:32], last))
    first = jnp.full((16, 128), core, jnp.int32) == 0
    keep_ref[0] = jnp.where(first, upper, lower)
    send_ref[0] = jnp.where(first, lower, upper)


def gram_partial(thickness, basis, snap):
    half = pltpu.VMEM((1, 16, 128), jnp.float32)
    return pl.pallas_call(
        gram_body,
        out_shape=(pltpu.VMEM((WIDE, 128), jnp.float32), half, half),
        in_specs=[smem()] + vmem(2),
        out_specs=vmem(3),
        scratch_shapes=[pltpu.VMEM((128, COLS), jnp.bfloat16)],
        compiler_params=pltpu.CompilerParams(vmem_limit_bytes=8 * MIB),
        cost_estimate=pl.CostEstimate(flops=10**9, transcendentals=0, bytes_accessed=10**7),
        name="gram",
    )(thickness, near(basis), near(snap))


def combine_body(*refs):
    *ins, out_ref = refs
    pieces = [ref[i] for ref in ins for i in range(ref.shape[0])]
    while len(pieces) > 1:
        pieces = [sum(pieces[i : i + 2]) for i in range(0, len(pieces), 2)]
    for i in range(out_ref.shape[0]):
        out_ref[i] = pieces[0]


def combine(arrays, copies):
    return pl.pallas_call(
        combine_body,
        out_shape=pltpu.VMEM((copies, 16, 128), jnp.float32),
        in_specs=vmem(len(arrays)),
        out_specs=vmem()[0],
        compiler_params=pltpu.CompilerParams(vmem_limit_bytes=MIB),
        name="combine",
    )(*(near(a) for a in arrays))


def update_body(mine_ref, other_ref, sv_ref, s0, s1, s2, s3, wide_ref, gram_ref, new_ref, off_ref, snap_ref, f_ref, out_ref, sems):
    g = lax.axis_index("grp")
    core = lax.axis_index("slab_2")
    slab = (lax.axis_index("slab_0") * 4 + lax.axis_index("slab_1")) * 2 + core
    place = g * 64 + slab
    for k, ref in enumerate((s0, s1, s2, s3)):
        snap_ref[g ^ k] = ref[...]
    mine, other = mine_ref[0], other_ref[0]
    first = jnp.full((16, 128), core, jnp.int32) == 0
    upper, lower = jnp.where(first, mine, other), jnp.where(first, other, mine)
    lane = lax.broadcasted_iota(jnp.int32, (16, 128), 1)
    row = lax.broadcasted_iota(jnp.int32, (16, 128), 0)
    order = row * 16 + lane
    thick = jnp.where(lane < 16, lower, 0.0)
    before = jnp.sum(jnp.where(order < place, thick, 0.0))
    off_ref[0, 0] = before.astype(jnp.int32)
    live = jnp.sum(thick) * PLANE
    blocks = (
        upper,
        lower,
        pltpu.roll(upper, 128 - 48, 1),
        pltpu.roll(lower, 128 - 32, 1),
        pltpu.roll(lower, 128 - 48, 1),
    )
    diag = [jnp.where((lane >= 16 * i) & (lane < 80), b, 0.0) for i, b in enumerate(blocks)]
    strict = [jnp.where(lane >= 16 * (i + 1), b, 0.0) for i, b in enumerate(diag)]
    pad = [jnp.zeros((48, 128), jnp.float32)]
    raw = jnp.concatenate(diag + pad, 0) + jnp.concatenate(strict + pad, 0).T
    scale_row = jnp.concatenate([sv_ref[...], jnp.ones((1, 128 - R), jnp.float32)], 1)
    scale_cols = jnp.broadcast_to(scale_row, (128, 128))
    scale_rows = scale_cols.T
    full = raw * scale_rows * scale_cols / (3.0 * live)
    gram_ref[...] = full[:N, :N]
    it = full[:R]
    it = it * (0.5 * R**0.5 / jnp.sqrt(jnp.sum(it * it)))
    for _ in range(4):
        prod = lax.dot_general(it, it, (((1,), (1,)), ((), ())), precision=HIGHEST)
        it = 1.5 * it - 0.5 * jnp.dot(prod, it, precision=HIGHEST)
    mix = (it * scale_cols[:R])[:, :N].astype(jnp.bfloat16)
    slab_thick = [
        jnp.sum(jnp.where(order == k * 64 + slab, thick, 0.0)).astype(jnp.int32) for k in range(G)
    ]
    copies = []
    for c in range(3):
        for k in range(G):
            tiles = range(c * 16, c * 16 + 16)
            parts = [wide_ref[pl.ds(j * G + k, R, stride=PITCH), :].astype(jnp.bfloat16) for j in tiles]
            snap = snap_ref[k, :, pl.ds(c * 2048, 2048)]
            stacked = jnp.concatenate([jnp.concatenate(parts, 1), snap], 0)
            res = jnp.dot(mix, stacked, preferred_element_type=jnp.float32)
            for t, j in enumerate(tiles):
                part = jnp.where(live_tile(t, slab_thick[k], R), res[:, t * 128 : (t + 1) * 128], 0.0)
                f_ref[pl.ds(j * G + k, R, stride=PITCH), :] = part

        def narrow(r, _):
            part = f_ref[pl.ds(r * PITCH + c * 64, 64), :]
            out_ref[r, pl.ds(c * 64, 64), :] = part.astype(jnp.bfloat16)
            return 0

        lax.fori_loop(0, R, narrow, 0, unroll=4)
        part = pl.ds(c * 64, 64)
        copy = pltpu.make_async_copy(out_ref.at[:, part], new_ref.at[:, part], sems.at[c])
        copy.start()
        copies.append(copy)
    for copy in copies:
        copy.wait()


def update(mine, other, sv, wide, snaps):
    return pl.pallas_call(
        update_body,
        out_shape=(
            jax.ShapeDtypeStruct((N, N), jnp.float32),
            jax.ShapeDtypeStruct((R, ROWS, 128), jnp.bfloat16),
            jax.ShapeDtypeStruct((1, 1), jnp.int32),
        ),
        in_specs=vmem(8),
        out_specs=(vmem()[0], pl.BlockSpec(memory_space=pl.ANY), smem()),
        scratch_shapes=[
            pltpu.VMEM((G, S, COLS), jnp.bfloat16),
            pltpu.VMEM((WIDE, 128), jnp.float32),
            pltpu.VMEM((R, ROWS, 128), jnp.bfloat16),
            pltpu.SemaphoreType.DMA((3,)),
        ],
        compiler_params=pltpu.CompilerParams(vmem_limit_bytes=20 * MIB),
        name="update",
    )(near(mine), near(other), near(sv.reshape(1, R)), *(near(s) for s in snaps), near(wide))


def from_region(snap, k):
    return lax.ppermute(snap, "grp", [(i, i ^ k) for i in range(G)])


def per_device(velocity, old_basis, singular_values, thickness):
    basis = old_basis.reshape(R, 3, G, 16, 128).transpose(0, 1, 3, 2, 4).reshape(R, ROWS, 128)
    snap = snapshots(thickness, velocity)
    snaps = [snap] + [from_region(snap, k) for k in (1, 2, 3)]
    wide, keep, send = gram_partial(thickness, basis, snap)
    swap = [(0, 1), (1, 0)]
    got = lax.ppermute(send, "slab_2", swap)
    for axis, size in (("slab_0", 8), (("grp", "slab_1"), 16)):
        spread = combine((keep, got) if size == 8 else (got,), size)
        got = lax.all_to_all(spread, axis, 0, 0, tiled=True)
    half = combine((got,), 1)
    other = lax.ppermute(half, "slab_2", swap)
    gram_matrix, new, offsets = update(half, other, singular_values, wide, snaps)
    new_basis = new.reshape(R, 3, 16, G, 128).transpose(0, 1, 3, 2, 4).reshape(R, 3, G, 2048)
    return (gram_matrix, new_basis, offsets)


def solution(mesh):
    split = Mesh(
        mesh.devices.reshape(mesh.shape["grp"], 8, 4, 2), ("grp", "slab_0", "slab_1", "slab_2")
    )
    in_specs = (P(None, None, "grp", SLAB), P(None, None, None, SLAB), P(), P("grp", SLAB))
    out_specs = (P(), P(None, None, None, SLAB), P("grp", SLAB))
    return jax.shard_map(
        per_device, mesh=split, in_specs=in_specs, out_specs=out_specs, check_vma=False
    )
```

profile of v0, /device:TPU:1, one launch (start us, length us, event | category | flops | bytes accessed | tf_op | source)
XLA Modules:
  0.0 51.2 jit_solution(15671671118117387843)
XLA Ops:
  1.3 0.0 copy-start.3
  1.3 1.3 %snapshots.1.snap_ref.s0 = bf16[16,6144]{1,0:T(8,128)(2,1)S(1)} custom-call(s32[1,1]{1,0:T(1,128)S(6)} %copy.9.thick_ref, f32[768,128]{1,0:T(8,128)} %bitcast.15), custom_call_target="tpu_custom_call" | custom-call | flops 2000000000 | bytes 1000000 | tf_op jit(solution)/shard_map/snapshots/pallas_call | solution.py:62
  2.6 0.0 copy-start.2
  2.6 0.7 %copy-done.3 = bf16[64,3,4,2048]{3,2,1,0:T(4,128)(2,1)S(1)} copy-done((bf16[64,3,4,2048]{3,2,1,0:T(4,128)(2,1)S(1)}, bf16[64,3,4,2048]{3,2,1,0:T(4,128)(2,1)}, u32[]{:S(2)}) %copy-start.3) | copy-done | bytes 3145752
  3.3 1.1 %gram.1 = (f32[12552,128]{1,0:T(8,128)S(1)}, f32[1,16,128]{2,1,0:T(8,128)S(1)}, f32[1,16,128]{2,1,0:T(8,128)S(1)}) custom-call(s32[1,1]{1,0:T(1,128)S(6)} %copy.9.thick_ref, bf16[64,192,128]{2,1,0:T(8,128)(2,1)S(1)} %bitcast.13, bf16[16,6144]{1,0:T(8,128)(2,1)S(1)} %snapshots.1.snap_ref.s0), custom_call_target="tpu_custom_call" | custom-call | flops 1000000000 | bytes 10000000 | tf_op jit(solution)/shard_map/gram/pallas_call | solution.py:108
  4.4 0.0 copy-start
  4.4 2.7 %copy-done = f32[12552,128]{1,0:T(8,128)} copy-done((f32[12552,128]{1,0:T(8,128)}, f32[12552,128]{1,0:T(8,128)S(1)}, u32[]{:S(2)}) %copy-start) | copy-done | bytes 6426648
  7.1 3.2 %collective-permute-start = (f32[1,16,128]{2,1,0:T(8,128)S(1)}, f32[1,16,128]{2,1,0:T(8,128)S(1)}, u32[]{:S(2)}, u32[]{:S(2)}) collective-permute-start(f32[1,16,128]{2,1,0:T(8,128)S(1)} %get-tuple-element.10), channel_id=1, source_target_pairs={{0,1},{1,0},{2,3},{3,2},{4,5},{5,4},{6,7},{7,6},{8,9},{9,8},{10,11... | collective-permute-start | bytes 24584 | tf_op jit(solution)/shard_map/ppermute | solution.py:239
  10.3 0.8 %collective-permute-done.refs_1_ = f32[1,16,128]{2,1,0:T(8,128)S(1)} collective-permute-done((f32[1,16,128]{2,1,0:T(8,128)S(1)}, f32[1,16,128]{2,1,0:T(8,128)S(1)}, u32[]{:S(2)}, u32[]{:S(2)}) %collective-permute-start) | collective-permute-done | bytes 8224 | tf_op jit(solution)/shard_map/ppermute | solution.py:239
  11.1 0.6 %combine.3 = f32[8,16,128]{2,1,0:T(8,128)} custom-call(f32[1,16,128]{2,1,0:T(8,128)S(1)} %get-tuple-element.9.refs_0_, f32[1,16,128]{2,1,0:T(8,128)S(1)} %collective-permute-done.refs_1_), custom_call_target="tpu_custom_call" | custom-call | tf_op jit(solution)/shard_map/combine/pallas_call | solution.py:130
  11.8 6.5 %all-to-all-start = ((f32[8,16,128]{2,1,0:T(8,128)}), f32[8,16,128]{2,1,0:T(8,128)S(1)}, u32[]{:S(2)}, u32[]{:S(2)}) async-start(f32[8,16,128]{2,1,0:T(8,128)} %combine.3), calls=%async_computation | async-start | bytes 131072 | tf_op jit(solution)/shard_map/all_to_all | solution.py:242
  18.3 2.7 %collective-permute-start.4 = (bf16[16,6144]{1,0:T(8,128)(2,1)S(1)}, bf16[16,6144]{1,0:T(8,128)(2,1)S(1)}, u32[]{:S(2)}, u32[]{:S(2)}) collective-permute-start(bf16[16,6144]{1,0:T(8,128)(2,1)S(1)} %snapshots.1.snap_ref.s0), channel_id=1, source_target_pairs={{0,192},{64,128},{128,64},{192,0},{1,193},{65,129},{129,65},{193,1... | collective-permute-start | bytes 589832 | tf_op jit(solution)/shard_map/ppermute | solution.py:230
  21.0 0.3 collective-permute-start.3
  21.3 0.3 collective-permute-start.2
  21.7 3.8 %all-to-all-done.refs_0_ = f32[8,16,128]{2,1,0:T(8,128)S(1)} async-done(((f32[8,16,128]{2,1,0:T(8,128)}), f32[8,16,128]{2,1,0:T(8,128)S(1)}, u32[]{:S(2)}, u32[]{:S(2)}) %all-to-all-start) | async-done | bytes 65568 | tf_op jit(solution)/shard_map/all_to_all | solution.py:242
  25.5 13.4 %all_to_all.10.refs_0_ = f32[16,16,128]{2,1,0:T(8,128)S(1)} all-to-all(f32[16,16,128]{2,1,0:T(8,128)S(1)} %combine.4), channel_id=1, replica_groups=mesh['grp'=4,'slab_0'=8,'slab_1'=4,'slab_2'=2] {'grp','slab_1'}, dimensions={0} | all-to-all | bytes 262144 | tf_op jit(solution)/shard_map/all_to_all | solution.py:242
  38.9 3.3 %collective-permute-start.1 = (f32[1,16,128]{2,1,0:T(8,128)S(1)}, f32[1,16,128]{2,1,0:T(8,128)S(1)}, u32[]{:S(2)}, u32[]{:S(2)}) collective-permute-start(f32[1,16,128]{2,1,0:T(8,128)S(1)} %combine.5.mine_ref), channel_id=1, source_target_pairs={{0,1},{1,0},{2,3},{3,2},{4,5},{5,4},{6,7},{7,6},{8,9},{9,8},{10,11... | collective-permute-start | bytes 24584 | tf_op jit(solution)/shard_map/ppermute | solution.py:244
  42.2 0.0 collective-permute-done.4.s3
  42.2 0.0 collective-permute-done.3.s2
  42.2 0.0 collective-permute-done.2.s1
  42.2 0.8 %collective-permute-done.1.other_ref = f32[1,16,128]{2,1,0:T(8,128)S(1)} collective-permute-done((f32[1,16,128]{2,1,0:T(8,128)S(1)}, f32[1,16,128]{2,1,0:T(8,128)S(1)}, u32[]{:S(2)}, u32[]{:S(2)}) %collective-permute-start.1) | collective-permute-done | bytes 8224 | tf_op jit(solution)/shard_map/ppermute | solution.py:244
  43.0 0.0 copy-done.2
  43.0 2.8 %copy-done.1 = f32[12552,128]{1,0:T(8,128)S(1)} copy-done((f32[12552,128]{1,0:T(8,128)S(1)}, f32[12552,128]{1,0:T(8,128)}, u32[]{:S(2)}) %copy-start.1) | copy-done | bytes 6426648
  45.9 5.3 %update.1 = (f32[80,80]{1,0:T(8,128)}, bf16[64,192,128]{2,1,0:T(8,128)(2,1)}, s32[1,1]{1,0:T(1,128)}) custom-call(f32[1,16,128]{2,1,0:T(8,128)S(1)} %combine.5.mine_ref, f32[1,16,128]{2,1,0:T(8,128)S(1)} %collective-permute-done.1.other_ref, f32[1,64]{1,0:T(1,128)S(1)} %bitcast.12, bf16[16,6144]{1,0:T(8,128)(2,1)S(1)} %snapshots.1.snap_ref.s0, ...), custom_call_target="tpu_custom_call" | custom-call | tf_op jit(solution)/shard_map/update/pallas_call | solution.py:209
  (3 shorter events, 0.0 us)
Async XLA Ops:
  1.3 2.0 %copy-start.3 = (bf16[64,3,4,2048]{3,2,1,0:T(4,128)(2,1)S(1)}, bf16[64,3,4,2048]{3,2,1,0:T(4,128)(2,1)}, u32[]{:S(2)}) copy-start(bf16[64,3,4,2048]{3,2,1,0:T(4,128)(2,1)} %param.5) | copy-start | bytes 9437188
  2.6 40.4 %copy-start.2 = (f32[64]{0:T(128)S(1)}, f32[64]{0:T(128)}, u32[]{:S(2)}) copy-start(f32[64]{0:T(128)} %param.6) | copy-start | bytes 772
  4.4 2.7 %copy-start = (f32[12552,128]{1,0:T(8,128)}, f32[12552,128]{1,0:T(8,128)S(1)}, u32[]{:S(2)}) copy-start(f32[12552,128]{1,0:T(8,128)S(1)} %get-tuple-element.11.wide_ref) | copy-start | bytes 19279876
  7.1 4.0 %collective-permute-start = (f32[1,16,128]{2,1,0:T(8,128)S(1)}, f32[1,16,128]{2,1,0:T(8,128)S(1)}, u32[]{:S(2)}, u32[]{:S(2)}) collective-permute-start(f32[1,16,128]{2,1,0:T(8,128)S(1)} %get-tuple-element.10), channel_id=1, source_target_pairs={{0,1},{1,0},{2,3},{3,2},{4,5},{5,4},{6,7},{7,6},{8,9},{9,8},{10,11... | collective-permute-start | bytes 24584 | tf_op jit(solution)/shard_map/ppermute | solution.py:239
  11.8 13.7 %all-to-all-start = ((f32[8,16,128]{2,1,0:T(8,128)}), f32[8,16,128]{2,1,0:T(8,128)S(1)}, u32[]{:S(2)}, u32[]{:S(2)}) async-start(f32[8,16,128]{2,1,0:T(8,128)} %combine.3), calls=%async_computation | async-start | bytes 131072 | tf_op jit(solution)/shard_map/all_to_all | solution.py:242
  18.3 23.9 %collective-permute-start.4 = (bf16[16,6144]{1,0:T(8,128)(2,1)S(1)}, bf16[16,6144]{1,0:T(8,128)(2,1)S(1)}, u32[]{:S(2)}, u32[]{:S(2)}) collective-permute-start(bf16[16,6144]{1,0:T(8,128)(2,1)S(1)} %snapshots.1.snap_ref.s0), channel_id=1, source_target_pairs={{0,192},{64,128},{128,64},{192,0},{1,193},{65,129},{129,65},{193,1... | collective-permute-start | bytes 589832 | tf_op jit(solution)/shard_map/ppermute | solution.py:230
  21.0 21.2 %collective-permute-start.3 = (bf16[16,6144]{1,0:T(8,128)(2,1)S(1)}, bf16[16,6144]{1,0:T(8,128)(2,1)S(1)}, u32[]{:S(2)}, u32[]{:S(2)}) collective-permute-start(bf16[16,6144]{1,0:T(8,128)(2,1)S(1)} %snapshots.1.snap_ref.s0), channel_id=1, source_target_pairs={{0,128},{64,192},{128,0},{192,64},{1,129},{65,193},{129,1},{193,65... | collective-permute-start | bytes 589832 | tf_op jit(solution)/shard_map/ppermute | solution.py:230
  21.3 20.9 %collective-permute-start.2 = (bf16[16,6144]{1,0:T(8,128)(2,1)S(1)}, bf16[16,6144]{1,0:T(8,128)(2,1)S(1)}, u32[]{:S(2)}, u32[]{:S(2)}) collective-permute-start(bf16[16,6144]{1,0:T(8,128)(2,1)S(1)} %snapshots.1.snap_ref.s0), channel_id=1, source_target_pairs={{0,64},{64,0},{128,192},{192,128},{1,65},{65,1},{129,193},{193,129... | collective-permute-start | bytes 589832 | tf_op jit(solution)/shard_map/ppermute | solution.py:230
  38.9 4.1 %collective-permute-start.1 = (f32[1,16,128]{2,1,0:T(8,128)S(1)}, f32[1,16,128]{2,1,0:T(8,128)S(1)}, u32[]{:S(2)}, u32[]{:S(2)}) collective-permute-start(f32[1,16,128]{2,1,0:T(8,128)S(1)} %combine.5.mine_ref), channel_id=1, source_target_pairs={{0,1},{1,0},{2,3},{3,2},{4,5},{5,4},{6,7},{7,6},{8,9},{9,8},{10,11... | collective-permute-start | bytes 24584 | tf_op jit(solution)/shard_map/ppermute | solution.py:244
  43.0 2.8 %copy-start.1 = (f32[12552,128]{1,0:T(8,128)S(1)}, f32[12552,128]{1,0:T(8,128)}, u32[]{:S(2)}) copy-start(f32[12552,128]{1,0:T(8,128)} %copy-done) | copy-start | bytes 19279876
where the time goes:
time: 51.4 us; the launch traced here: 51.2 us
  starting transfers between devices  16.4 us (32%)
  blocking collectives  13.4 us (26%)
  Pallas kernels  8.42 us (16%)
  local copies, waits for them, and re-layouts  6.21 us (12%)
  waiting for transfers between devices  5.47 us (11%)
  between operations  1.32 us (3%)
    all_to_all x1, blocking collectives, per_device(): got = lax.all_to_all(spread, axis, 0, 0, tiled=True)  13.4 us
    all_to_all x1, starting transfers between devices, per_device(): got = lax.all_to_all(spread, axis, 0, 0, tiled=True)  6.48 us
    unnamed x8, local copies, waits for them, and re-layouts  6.21 us
    pallas_call x1, Pallas kernels, update(): pl.pallas_call(update_body, out_shape=(jax.ShapeDtypeStruct((N, N), jnp.f...  5.34 us
    all_to_all x1, waiting for transfers between devices, per_device(): got = lax.all_to_all(spread, axis, 0, 0, tiled=True)  3.82 us
    ppermute x3, starting transfers between devices, from_region(): return lax.ppermute(snap, 'grp', [(i, i ^ k) for i in range(G)])  3.41 us
    ppermute x1, starting transfers between devices, per_device(): other = lax.ppermute(half, 'slab_2', swap)  3.28 us
    ppermute x1, starting transfers between devices, per_device(): got = lax.ppermute(send, 'slab_2', swap)  3.2 us
  transfers between devices with their start and end apart: 6, of which 3 were waited for; matrix products, arithmetic and copies ran while one was open for 0% of the time, Pallas kernels for 0%

commit v1 on v0

--- a/solution.py
+++ b/solution.py
@@ -17,6 +17,7 @@
 COLS = 6144
 J = 48
 ROWS = 192
+VPITCH = J + 8
 PITCH = ROWS + 1
 WIDE = (R + 1) * PITCH + 7
 HIGHEST = lax.Precision.HIGHEST
@@ -47,31 +48,30 @@
     return jnp.full((rows, 128), jnp.where(t // 4 < thick, 1, 0), jnp.int32) > 0
 
 
-def snapshots_body(thick_ref, vel_hbm, snap_ref, vel_ref, sem):
-    get = pltpu.make_async_copy(vel_hbm, vel_ref, sem)
+def snapshots_body(vel_hbm, snap_ref, vel_ref, sem):
+    get = pltpu.make_async_copy(vel_hbm, vel_ref.at[:, 0:J], sem)
     get.start()
     get.wait()
-    thick = thick_ref[0, 0]
+    rows_ref = vel_ref.reshape(S * VPITCH, 128)
     for j in range(J):
-        rows = vel_ref[pl.ds(j, S, stride=J), :]
-        rows = jnp.where(live_tile(j % 16, thick, S), rows, 0.0)
+        rows = rows_ref[pl.ds(j, S, stride=VPITCH), :]
         snap_ref[:, pl.ds(j * 128, 128)] = rows.astype(jnp.bfloat16)
 
 
-def snapshots(thickness, velocity):
+def snapshots(velocity):
     return pl.pallas_call(
         snapshots_body,
         out_shape=pltpu.VMEM((S, COLS), jnp.bfloat16),
-        in_specs=[smem()] + hbm(),
+        in_specs=hbm(),
         out_specs=vmem()[0],
-        scratch_shapes=[pltpu.VMEM((S * J, 128), jnp.float32), pltpu.SemaphoreType.DMA(())],
+        scratch_shapes=[pltpu.VMEM((S, VPITCH, 128), jnp.float32), pltpu.SemaphoreType.DMA(())],
         compiler_params=pltpu.CompilerParams(vmem_limit_bytes=2 * MIB),
         cost_estimate=pl.CostEstimate(flops=2 * 10**9, transcendentals=0, bytes_accessed=10**6),
         name="snapshots",
-    )(thickness, far(velocity.reshape(S * J, 128)))
-
-
-def gram_body(thick_ref, basis_ref, snap_ref, wide_ref, keep_ref, send_ref, stack_ref):
+    )(far(velocity.reshape(S, J, 128)))
+
+
+def gram_body(thick_ref, basis_ref, snap_ref, wide_ref, part_ref, stack_ref):
     g = lax.axis_index("grp")
     core = lax.axis_index("slab_2")
     place = ((g * 8 + lax.axis_index("slab_0")) * 4 + lax.axis_index("slab_1")) * 2 + core
@@ -86,7 +86,9 @@
         rows = wide_ref[pl.ds(j * G + g, R, stride=PITCH), :]
         rows = jnp.where(live_tile(j % 16, thick, R), rows, 0.0)
         stack_ref[0:R, pl.ds(j * 128, 128)] = rows.astype(jnp.bfloat16)
-    stack_ref[R:N, :] = snap_ref[...]
+        stack_ref[R:N, pl.ds(j * 128, 128)] = jnp.where(
+            live_tile(j % 16, thick, S), snap_ref[:, pl.ds(j * 128, 128)], jnp.zeros((), jnp.bfloat16)
+        )
     stack_ref[N:, :] = jnp.zeros((128 - N, COLS), jnp.bfloat16)
     stacked = stack_ref[...]
     gram = lax.dot_general(
@@ -98,18 +100,16 @@
     upper = jnp.where(lane < 80, gram[0:16], pltpu.roll(gram[32:48], 48, 1))
     last = jnp.where(lane < 112, pltpu.roll(gram[48:64], 32, 1), pltpu.roll(gram[64:80], 48, 1))
     lower = jnp.where(lane < 16, thick_block, jnp.where(lane < 80, gram[16:32], last))
-    first = jnp.full((16, 128), core, jnp.int32) == 0
-    keep_ref[0] = jnp.where(first, upper, lower)
-    send_ref[0] = jnp.where(first, lower, upper)
+    part_ref[0, 0:16] = upper
+    part_ref[0, 16:32] = lower
 
 
 def gram_partial(thickness, basis, snap):
-    half = pltpu.VMEM((1, 16, 128), jnp.float32)
     return pl.pallas_call(
         gram_body,
-        out_shape=(pltpu.VMEM((WIDE, 128), jnp.float32), half, half),
+        out_shape=(pltpu.VMEM((WIDE, 128), jnp.float32), pltpu.VMEM((1, 32, 128), jnp.float32)),
         in_specs=[smem()] + vmem(2),
-        out_specs=vmem(3),
+        out_specs=vmem(2),
         scratch_shapes=[pltpu.VMEM((128, COLS), jnp.bfloat16)],
         compiler_params=pltpu.CompilerParams(vmem_limit_bytes=8 * MIB),
         cost_estimate=pl.CostEstimate(flops=10**9, transcendentals=0, bytes_accessed=10**7),
@@ -117,19 +117,24 @@
     )(thickness, near(basis), near(snap))
 
 
+def tree_sum(pieces):
+    while len(pieces) > 1:
+        pieces = [sum(pieces[i + 1 : i + 2], pieces[i]) for i in range(0, len(pieces), 2)]
+    return pieces[0]
+
+
 def combine_body(*refs):
     *ins, out_ref = refs
     pieces = [ref[i] for ref in ins for i in range(ref.shape[0])]
-    while len(pieces) > 1:
-        pieces = [sum(pieces[i : i + 2]) for i in range(0, len(pieces), 2)]
+    total = tree_sum(pieces)
     for i in range(out_ref.shape[0]):
-        out_ref[i] = pieces[0]
+        out_ref[i] = total
 
 
 def combine(arrays, copies):
     return pl.pallas_call(
         combine_body,
-        out_shape=pltpu.VMEM((copies, 16, 128), jnp.float32),
+        out_shape=pltpu.VMEM((copies, 32, 128), jnp.float32),
         in_specs=vmem(len(arrays)),
         out_specs=vmem()[0],
         compiler_params=pltpu.CompilerParams(vmem_limit_bytes=MIB),
@@ -137,16 +142,14 @@
     )(*(near(a) for a in arrays))
 
 
-def update_body(mine_ref, other_ref, sv_ref, s0, s1, s2, s3, wide_ref, gram_ref, new_ref, off_ref, snap_ref, f_ref, out_ref, sems):
+def update_body(total_ref, sv_ref, s0, s1, s2, s3, wide_ref, gram_ref, new_ref, off_ref, snap_ref, f_ref, out_ref, sems):
     g = lax.axis_index("grp")
     core = lax.axis_index("slab_2")
     slab = (lax.axis_index("slab_0") * 4 + lax.axis_index("slab_1")) * 2 + core
     place = g * 64 + slab
     for k, ref in enumerate((s0, s1, s2, s3)):
         snap_ref[g ^ k] = ref[...]
-    mine, other = mine_ref[0], other_ref[0]
-    first = jnp.full((16, 128), core, jnp.int32) == 0
-    upper, lower = jnp.where(first, mine, other), jnp.where(first, other, mine)
+    upper, lower = total_ref[0, 0:16], total_ref[0, 16:32]
     lane = lax.broadcasted_iota(jnp.int32, (16, 128), 1)
     row = lax.broadcasted_iota(jnp.int32, (16, 128), 0)
     order = row * 16 + lane
@@ -205,7 +208,7 @@
         copy.wait()
 
 
-def update(mine, other, sv, wide, snaps):
+def update(total, sv, wide, snaps):
     return pl.pallas_call(
         update_body,
         out_shape=(
@@ -213,7 +216,7 @@
             jax.ShapeDtypeStruct((R, ROWS, 128), jnp.bfloat16),
             jax.ShapeDtypeStruct((1, 1), jnp.int32),
         ),
-        in_specs=vmem(8),
+        in_specs=vmem(7),
         out_specs=(vmem()[0], pl.BlockSpec(memory_space=pl.ANY), smem()),
         scratch_shapes=[
             pltpu.VMEM((G, S, COLS), jnp.bfloat16),
@@ -223,7 +226,7 @@
         ],
         compiler_params=pltpu.CompilerParams(vmem_limit_bytes=20 * MIB),
         name="update",
-    )(near(mine), near(other), near(sv.reshape(1, R)), *(near(s) for s in snaps), near(wide))
+    )(near(total), near(sv.reshape(1, R)), *(near(s) for s in snaps), near(wide))
 
 
 def from_region(snap, k):
@@ -232,17 +235,16 @@
 
 def per_device(velocity, old_basis, singular_values, thickness):
     basis = old_basis.reshape(R, 3, G, 16, 128).transpose(0, 1, 3, 2, 4).reshape(R, ROWS, 128)
-    snap = snapshots(thickness, velocity)
+    snap = snapshots(velocity)
+    thickness = lax.optimization_barrier((thickness, snap))[0]
     snaps = [snap] + [from_region(snap, k) for k in (1, 2, 3)]
-    wide, keep, send = gram_partial(thickness, basis, snap)
-    swap = [(0, 1), (1, 0)]
-    got = lax.ppermute(send, "slab_2", swap)
+    wide, part = gram_partial(thickness, basis, snap)
+    got = lax.ppermute(part, "slab_2", [(0, 1), (1, 0)])
     for axis, size in (("slab_0", 8), (("grp", "slab_1"), 16)):
-        spread = combine((keep, got) if size == 8 else (got,), size)
+        spread = combine((part, got) if size == 8 else (got,), size)
         got = lax.all_to_all(spread, axis, 0, 0, tiled=True)
-    half = combine((got,), 1)
-    other = lax.ppermute(half, "slab_2", swap)
-    gram_matrix, new, offsets = update(half, other, singular_values, wide, snaps)
+    total = combine((got,), 1)
+    gram_matrix, new, offsets = update(total, singular_values, wide, snaps)
     new_basis = new.reshape(R, 3, 16, G, 128).transpose(0, 1, 3, 2, 4).reshape(R, 3, G, 2048)
     return (gram_matrix, new_basis, offsets)
 

time: 51.4 us -> 55.5 us (1.080)
  the two profiles are of different devices: /device:TPU:1 before, /device:TPU:6 now
where the time goes in v1:
time: 55.5 us; the launch traced here: 55.2 us
  blocking collectives  17.7 us (32%)
  starting transfers between devices  11.5 us (21%)
  waiting for transfers between devices  9.91 us (18%)
  Pallas kernels  8.46 us (15%)
  local copies, waits for them, and re-layouts  6.29 us (11%)
  between operations  1.33 us (2%)
    all_to_all x1, blocking collectives, per_device(): got = lax.all_to_all(spread, axis, 0, 0, tiled=True)  17.7 us
    all_to_all x1, starting transfers between devices, per_device(): got = lax.all_to_all(spread, axis, 0, 0, tiled=True)  7.43 us
    unnamed x8, local copies, waits for them, and re-layouts  6.29 us
    pallas_call x1, Pallas kernels, update(): pl.pallas_call(update_body, out_shape=(jax.ShapeDtypeStruct((N, N), jnp.f...  5.34 us
    ppermute x3, waiting for transfers between devices, from_region(): return lax.ppermute(snap, 'grp', [(i, i ^ k) for i in range(G)])  4.46 us
    all_to_all x1, waiting for transfers between devices, per_device(): got = lax.all_to_all(spread, axis, 0, 0, tiled=True)  4.26 us
    ppermute x3, starting transfers between devices, from_region(): return lax.ppermute(snap, 'grp', [(i, i ^ k) for i in range(G)])  4.09 us
    pallas_call x1, Pallas kernels, snapshots(): pl.pallas_call(snapshots_body, out_shape=pltpu.VMEM((S, COLS), jnp.bfloat...  1.23 us
  transfers between devices with their start and end apart: 5, of which 3 were waited for; matrix products, arithmetic and copies ran while one was open for 0% of the time, Pallas kernels for 0%

profile of v1, /device:TPU:6, one launch (start us, length us, event | category | flops | bytes accessed | tf_op | source)
XLA Modules:
  0.0 55.2 jit_solution(13157489616397816035)
XLA Ops:
  1.3 0.0 copy-start.3
  1.3 1.2 %snapshots.1.snap_ref.s0 = bf16[16,6144]{1,0:T(8,128)(2,1)S(1)} custom-call(f32[16,48,128]{2,1,0:T(8,128)} %bitcast.15), custom_call_target="tpu_custom_call" | custom-call | flops 2000000000 | bytes 1000000 | tf_op jit(solution)/shard_map/snapshots/pallas_call | solution.py:62
  2.5 0.0 copy-start.2
  2.5 0.7 %copy-done.3 = bf16[64,3,4,2048]{3,2,1,0:T(4,128)(2,1)S(1)} copy-done((bf16[64,3,4,2048]{3,2,1,0:T(4,128)(2,1)S(1)}, bf16[64,3,4,2048]{3,2,1,0:T(4,128)(2,1)}, u32[]{:S(2)}) %copy-start.3) | copy-done | bytes 3145752
  3.3 1.1 %gram.1 = (f32[12552,128]{1,0:T(8,128)S(1)}, f32[1,32,128]{2,1,0:T(8,128)S(1)}) custom-call(s32[1,1]{1,0:T(1,128)S(6)} %copy.9.thick_ref, bf16[64,192,128]{2,1,0:T(8,128)(2,1)S(1)} %bitcast.13, bf16[16,6144]{1,0:T(8,128)(2,1)S(1)} %snapshots.1.snap_ref.s0), custom_call_target="tpu_custom_call" | custom-call | flops 1000000000 | bytes 10000000 | tf_op jit(solution)/shard_map/gram/pallas_call | solution.py:108
  4.4 0.0 copy-start
  4.4 2.7 %copy-done = f32[12552,128]{1,0:T(8,128)} copy-done((f32[12552,128]{1,0:T(8,128)}, f32[12552,128]{1,0:T(8,128)S(1)}, u32[]{:S(2)}) %copy-start) | copy-done | bytes 6426648
  7.1 0.0 collective-permute-start
  7.1 1.2 %collective-permute-done.refs_1_ = f32[1,32,128]{2,1,0:T(8,128)S(1)} collective-permute-done((f32[1,32,128]{2,1,0:T(8,128)S(1)}, f32[1,32,128]{2,1,0:T(8,128)S(1)}, u32[]{:S(2)}, u32[]{:S(2)}) %collective-permute-start) | collective-permute-done | bytes 16416 | tf_op jit(solution)/shard_map/ppermute | solution.py:242
  8.3 17.7 %all_to_all.10.refs_0_ = f32[8,32,128]{2,1,0:T(8,128)S(1)} all-to-all(f32[8,32,128]{2,1,0:T(8,128)S(1)} %combine.3), channel_id=1, replica_groups=mesh['grp'=4,'slab_0'=8,'slab_1'=4,'slab_2'=2] {'slab_0'}, dimensions={0} | all-to-all | bytes 262144 | tf_op jit(solution)/shard_map/all_to_all | solution.py:245
  26.0 0.7 %combine.4 = f32[16,32,128]{2,1,0:T(8,128)} custom-call(f32[8,32,128]{2,1,0:T(8,128)S(1)} %all_to_all.10.refs_0_), custom_call_target="tpu_custom_call" | custom-call | tf_op jit(solution)/shard_map/combine/pallas_call | solution.py:135
  26.7 7.4 %all-to-all-start.1 = ((f32[16,32,128]{2,1,0:T(8,128)}), f32[16,32,128]{2,1,0:T(8,128)S(1)}, u32[]{:S(2)}, u32[]{:S(2)}) async-start(f32[16,32,128]{2,1,0:T(8,128)} %combine.4), calls=%async_computation.1 | async-start | bytes 524288 | tf_op jit(solution)/shard_map/all_to_all | solution.py:245
  34.1 2.7 %collective-permute-start.3 = (bf16[16,6144]{1,0:T(8,128)(2,1)S(1)}, bf16[16,6144]{1,0:T(8,128)(2,1)S(1)}, u32[]{:S(2)}, u32[]{:S(2)}) collective-permute-start(bf16[16,6144]{1,0:T(8,128)(2,1)S(1)} %snapshots.1.snap_ref.s0), channel_id=1, source_target_pairs={{0,192},{64,128},{128,64},{192,0},{1,193},{65,129},{129,65},{193,1... | collective-permute-start | bytes 589832 | tf_op jit(solution)/shard_map/ppermute | solution.py:233
  36.8 0.9 %collective-permute-start.2 = (bf16[16,6144]{1,0:T(8,128)(2,1)S(1)}, bf16[16,6144]{1,0:T(8,128)(2,1)S(1)}, u32[]{:S(2)}, u32[]{:S(2)}) collective-permute-start(bf16[16,6144]{1,0:T(8,128)(2,1)S(1)} %snapshots.1.snap_ref.s0), channel_id=1, source_target_pairs={{0,128},{64,192},{128,0},{192,64},{1,129},{65,193},{129,1},{193,65... | collective-permute-start | bytes 589832 | tf_op jit(solution)/shard_map/ppermute | solution.py:233
  37.7 0.6 %collective-permute-start.1 = (bf16[16,6144]{1,0:T(8,128)(2,1)S(1)}, bf16[16,6144]{1,0:T(8,128)(2,1)S(1)}, u32[]{:S(2)}, u32[]{:S(2)}) collective-permute-start(bf16[16,6144]{1,0:T(8,128)(2,1)S(1)} %snapshots.1.snap_ref.s0), channel_id=1, source_target_pairs={{0,64},{64,0},{128,192},{192,128},{1,65},{65,1},{129,193},{193,129... | collective-permute-start | bytes 589832 | tf_op jit(solution)/shard_map/ppermute | solution.py:233
  38.2 4.3 %all-to-all-done.1.refs_0_ = f32[16,32,128]{2,1,0:T(8,128)S(1)} async-done(((f32[16,32,128]{2,1,0:T(8,128)}), f32[16,32,128]{2,1,0:T(8,128)S(1)}, u32[]{:S(2)}, u32[]{:S(2)}) %all-to-all-start.1) | async-done | bytes 262176 | tf_op jit(solution)/shard_map/all_to_all | solution.py:245
  42.5 4.5 %collective-permute-done.3.s3 = bf16[16,6144]{1,0:T(8,128)(2,1)S(1)} collective-permute-done((bf16[16,6144]{1,0:T(8,128)(2,1)S(1)}, bf16[16,6144]{1,0:T(8,128)(2,1)S(1)}, u32[]{:S(2)}, u32[]{:S(2)}) %collective-permute-start.3) | collective-permute-done | bytes 196640 | tf_op jit(solution)/shard_map/ppermute | solution.py:233
  47.0 0.0 collective-permute-done.2.s2
  47.0 0.0 collective-permute-done.1.s1
  47.0 0.0 copy-done.2
  47.0 0.0 copy-start.1
  47.0 2.8 %copy-done.1 = f32[12552,128]{1,0:T(8,128)S(1)} copy-done((f32[12552,128]{1,0:T(8,128)S(1)}, f32[12552,128]{1,0:T(8,128)}, u32[]{:S(2)}) %copy-start.1) | copy-done | bytes 6426648
  49.8 5.3 %update.1 = (f32[80,80]{1,0:T(8,128)}, bf16[64,192,128]{2,1,0:T(8,128)(2,1)}, s32[1,1]{1,0:T(1,128)}) custom-call(f32[1,32,128]{2,1,0:T(8,128)S(1)} %combine.5.total_ref, f32[1,64]{1,0:T(1,128)S(1)} %bitcast.12, bf16[16,6144]{1,0:T(8,128)(2,1)S(1)} %snapshots.1.snap_ref.s0, bf16[16,6144]{1,0:T(8,128)(2,1)S(1)} %collective-permute-done.1.s1, ...), custom_call_target="tpu_custom_call" | custom-call | tf_op jit(solution)/shard_map/update/pallas_call | solution.py:212
  (2 shorter events, 0.0 us)
Async XLA Ops:
  1.3 2.0 %copy-start.3 = (bf16[64,3,4,2048]{3,2,1,0:T(4,128)(2,1)S(1)}, bf16[64,3,4,2048]{3,2,1,0:T(4,128)(2,1)}, u32[]{:S(2)}) copy-start(bf16[64,3,4,2048]{3,2,1,0:T(4,128)(2,1)} %param.5) | copy-start | bytes 9437188
  2.5 44.5 %copy-start.2 = (f32[64]{0:T(128)S(1)}, f32[64]{0:T(128)}, u32[]{:S(2)}) copy-start(f32[64]{0:T(128)} %param.6) | copy-start | bytes 772
  4.4 2.7 %copy-start = (f32[12552,128]{1,0:T(8,128)}, f32[12552,128]{1,0:T(8,128)S(1)}, u32[]{:S(2)}) copy-start(f32[12552,128]{1,0:T(8,128)S(1)} %get-tuple-element.11.wide_ref) | copy-start | bytes 19279876
  7.1 1.2 %collective-permute-start = (f32[1,32,128]{2,1,0:T(8,128)S(1)}, f32[1,32,128]{2,1,0:T(8,128)S(1)}, u32[]{:S(2)}, u32[]{:S(2)}) collective-permute-start(f32[1,32,128]{2,1,0:T(8,128)S(1)} %get-tuple-element.10.refs_0_), channel_id=1, source_target_pairs={{0,1},{1,0},{2,3},{3,2},{4,5},{5,4},{6,7},{7,6},{8,9},{9,8},{10,11... | collective-permute-start | bytes 49160 | tf_op jit(solution)/shard_map/ppermute | solution.py:242
  26.7 15.8 %all-to-all-start.1 = ((f32[16,32,128]{2,1,0:T(8,128)}), f32[16,32,128]{2,1,0:T(8,128)S(1)}, u32[]{:S(2)}, u32[]{:S(2)}) async-start(f32[16,32,128]{2,1,0:T(8,128)} %combine.4), calls=%async_computation.1 | async-start | bytes 524288 | tf_op jit(solution)/shard_map/all_to_all | solution.py:245
  34.1 12.8 %collective-permute-start.3 = (bf16[16,6144]{1,0:T(8,128)(2,1)S(1)}, bf16[16,6144]{1,0:T(8,128)(2,1)S(1)}, u32[]{:S(2)}, u32[]{:S(2)}) collective-permute-start(bf16[16,6144]{1,0:T(8,128)(2,1)S(1)} %snapshots.1.snap_ref.s0), channel_id=1, source_target_pairs={{0,192},{64,128},{128,64},{192,0},{1,193},{65,129},{129,65},{193,1... | collective-permute-start | bytes 589832 | tf_op jit(solution)/shard_map/ppermute | solution.py:233
  36.8 10.2 %collective-permute-start.2 = (bf16[16,6144]{1,0:T(8,128)(2,1)S(1)}, bf16[16,6144]{1,0:T(8,128)(2,1)S(1)}, u32[]{:S(2)}, u32[]{:S(2)}) collective-permute-start(bf16[16,6144]{1,0:T(8,128)(2,1)S(1)} %snapshots.1.snap_ref.s0), channel_id=1, source_target_pairs={{0,128},{64,192},{128,0},{192,64},{1,129},{65,193},{129,1},{193,65... | collective-permute-start | bytes 589832 | tf_op jit(solution)/shard_map/ppermute | solution.py:233
  37.7 9.3 %collective-permute-start.1 = (bf16[16,6144]{1,0:T(8,128)(2,1)S(1)}, bf16[16,6144]{1,0:T(8,128)(2,1)S(1)}, u32[]{:S(2)}, u32[]{:S(2)}) collective-permute-start(bf16[16,6144]{1,0:T(8,128)(2,1)S(1)} %snapshots.1.snap_ref.s0), channel_id=1, source_target_pairs={{0,64},{64,0},{128,192},{192,128},{1,65},{65,1},{129,193},{193,129... | collective-permute-start | bytes 589832 | tf_op jit(solution)/shard_map/ppermute | solution.py:233
  47.0 2.8 %copy-start.1 = (f32[12552,128]{1,0:T(8,128)S(1)}, f32[12552,128]{1,0:T(8,128)}, u32[]{:S(2)}) copy-start(f32[12552,128]{1,0:T(8,128)} %copy-done) | copy-start | bytes 19279876

commit v2 on v1

--- a/solution.py
+++ b/solution.py
@@ -240,9 +240,9 @@
     snaps = [snap] + [from_region(snap, k) for k in (1, 2, 3)]
     wide, part = gram_partial(thickness, basis, snap)
     got = lax.ppermute(part, "slab_2", [(0, 1), (1, 0)])
-    for axis, size in (("slab_0", 8), (("grp", "slab_1"), 16)):
-        spread = combine((part, got) if size == 8 else (got,), size)
-        got = lax.all_to_all(spread, axis, 0, 0, tiled=True)
+    spread = combine((part, got), 8)
+    got = lax.all_to_all(spread, "slab_0", 0, 0, tiled=True)
+    got = lax.all_to_all(combine((got,), 16), ("grp", "slab_1"), 0, 0, tiled=True)
     total = combine((got,), 1)
     gram_matrix, new, offsets = update(total, singular_values, wide, snaps)
     new_basis = new.reshape(R, 3, 16, G, 128).transpose(0, 1, 3, 2, 4).reshape(R, 3, G, 2048)

time: 55.5 us -> 55.5 us (level)
  no operation moved by 1% of the time
where the time goes in v2:
time: 55.5 us; the launch traced here: 55.2 us
  blocking collectives  17.7 us (32%)
  starting transfers between devices  11.5 us (21%)
  waiting for transfers between devices  9.91 us (18%)
  Pallas kernels  8.46 us (15%)
  local copies, waits for them, and re-layouts  6.29 us (11%)
  between operations  1.33 us (2%)
    all_to_all x1, blocking collectives, per_device(): got = lax.all_to_all(spread, 'slab_0', 0, 0, tiled=True)  17.7 us
    all_to_all x1, starting transfers between devices, per_device(): lax.all_to_all(combine((got,), 16), ('grp', 'slab_1'), 0, 0, tiled=True)  7.43 us
    unnamed x8, local copies, waits for them, and re-layouts  6.29 us
    pallas_call x1, Pallas kernels, update(): pl.pallas_call(update_body, out_shape=(jax.ShapeDtypeStruct((N, N), jnp.f...  5.34 us
    ppermute x3, waiting for transfers between devices, from_region(): return lax.ppermute(snap, 'grp', [(i, i ^ k) for i in range(G)])  4.46 us
    all_to_all x1, waiting for transfers between devices, per_device(): lax.all_to_all(combine((got,), 16), ('grp', 'slab_1'), 0, 0, tiled=True)  4.26 us
    ppermute x3, starting transfers between devices, from_region(): return lax.ppermute(snap, 'grp', [(i, i ^ k) for i in range(G)])  4.09 us
    pallas_call x1, Pallas kernels, snapshots(): pl.pallas_call(snapshots_body, out_shape=pltpu.VMEM((S, COLS), jnp.bfloat...  1.23 us
  transfers between devices with their start and end apart: 5, of which 3 were waited for; matrix products, arithmetic and copies ran while one was open for 0% of the time, Pallas kernels for 0%

profile of v2, /device:TPU:6, one launch (start us, length us, event | category | flops | bytes accessed | tf_op | source)
XLA Modules:
  0.0 55.2 jit_solution(13157489616397816035)
XLA Ops:
  1.3 0.0 copy-start.3
  1.3 1.2 %snapshots.1.snap_ref.s0 = bf16[16,6144]{1,0:T(8,128)(2,1)S(1)} custom-call(f32[16,48,128]{2,1,0:T(8,128)} %bitcast.15), custom_call_target="tpu_custom_call" | custom-call | flops 2000000000 | bytes 1000000 | tf_op jit(solution)/shard_map/snapshots/pallas_call | solution.py:62
  2.5 0.0 copy-start.2
  2.5 0.7 %copy-done.3 = bf16[64,3,4,2048]{3,2,1,0:T(4,128)(2,1)S(1)} copy-done((bf16[64,3,4,2048]{3,2,1,0:T(4,128)(2,1)S(1)}, bf16[64,3,4,2048]{3,2,1,0:T(4,128)(2,1)}, u32[]{:S(2)}) %copy-start.3) | copy-done | bytes 3145752
  3.3 1.1 %gram.1 = (f32[12552,128]{1,0:T(8,128)S(1)}, f32[1,32,128]{2,1,0:T(8,128)S(1)}) custom-call(s32[1,1]{1,0:T(1,128)S(6)} %copy.9.thick_ref, bf16[64,192,128]{2,1,0:T(8,128)(2,1)S(1)} %bitcast.13, bf16[16,6144]{1,0:T(8,128)(2,1)S(1)} %snapshots.1.snap_ref.s0), custom_call_target="tpu_custom_call" | custom-call | flops 1000000000 | bytes 10000000 | tf_op jit(solution)/shard_map/gram/pallas_call | solution.py:108
  4.4 0.0 copy-start
  4.4 2.7 %copy-done = f32[12552,128]{1,0:T(8,128)} copy-done((f32[12552,128]{1,0:T(8,128)}, f32[12552,128]{1,0:T(8,128)S(1)}, u32[]{:S(2)}) %copy-start) | copy-done | bytes 6426648
  7.1 0.0 collective-permute-start
  7.1 1.2 %collective-permute-done.refs_1_ = f32[1,32,128]{2,1,0:T(8,128)S(1)} collective-permute-done((f32[1,32,128]{2,1,0:T(8,128)S(1)}, f32[1,32,128]{2,1,0:T(8,128)S(1)}, u32[]{:S(2)}, u32[]{:S(2)}) %collective-permute-start) | collective-permute-done | bytes 16416 | tf_op jit(solution)/shard_map/ppermute | solution.py:242
  8.3 17.7 %all_to_all.10.refs_0_ = f32[8,32,128]{2,1,0:T(8,128)S(1)} all-to-all(f32[8,32,128]{2,1,0:T(8,128)S(1)} %combine.3), channel_id=1, replica_groups=mesh['grp'=4,'slab_0'=8,'slab_1'=4,'slab_2'=2] {'slab_0'}, dimensions={0} | all-to-all | bytes 262144 | tf_op jit(solution)/shard_map/all_to_all | solution.py:244
  26.0 0.7 %combine.4 = f32[16,32,128]{2,1,0:T(8,128)} custom-call(f32[8,32,128]{2,1,0:T(8,128)S(1)} %all_to_all.10.refs_0_), custom_call_target="tpu_custom_call" | custom-call | tf_op jit(solution)/shard_map/combine/pallas_call | solution.py:135
  26.7 7.4 %all-to-all-start.1 = ((f32[16,32,128]{2,1,0:T(8,128)}), f32[16,32,128]{2,1,0:T(8,128)S(1)}, u32[]{:S(2)}, u32[]{:S(2)}) async-start(f32[16,32,128]{2,1,0:T(8,128)} %combine.4), calls=%async_computation.1 | async-start | bytes 524288 | tf_op jit(solution)/shard_map/all_to_all | solution.py:245
  34.1 2.7 %collective-permute-start.3 = (bf16[16,6144]{1,0:T(8,128)(2,1)S(1)}, bf16[16,6144]{1,0:T(8,128)(2,1)S(1)}, u32[]{:S(2)}, u32[]{:S(2)}) collective-permute-start(bf16[16,6144]{1,0:T(8,128)(2,1)S(1)} %snapshots.1.snap_ref.s0), channel_id=1, source_target_pairs={{0,192},{64,128},{128,64},{192,0},{1,193},{65,129},{129,65},{193,1... | collective-permute-start | bytes 589832 | tf_op jit(solution)/shard_map/ppermute | solution.py:233
  36.8 0.9 %collective-permute-start.2 = (bf16[16,6144]{1,0:T(8,128)(2,1)S(1)}, bf16[16,6144]{1,0:T(8,128)(2,1)S(1)}, u32[]{:S(2)}, u32[]{:S(2)}) collective-permute-start(bf16[16,6144]{1,0:T(8,128)(2,1)S(1)} %snapshots.1.snap_ref.s0), channel_id=1, source_target_pairs={{0,128},{64,192},{128,0},{192,64},{1,129},{65,193},{129,1},{193,65... | collective-permute-start | bytes 589832 | tf_op jit(solution)/shard_map/ppermute | solution.py:233
  37.7 0.6 %collective-permute-start.1 = (bf16[16,6144]{1,0:T(8,128)(2,1)S(1)}, bf16[16,6144]{1,0:T(8,128)(2,1)S(1)}, u32[]{:S(2)}, u32[]{:S(2)}) collective-permute-start(bf16[16,6144]{1,0:T(8,128)(2,1)S(1)} %snapshots.1.snap_ref.s0), channel_id=1, source_target_pairs={{0,64},{64,0},{128,192},{192,128},{1,65},{65,1},{129,193},{193,129... | collective-permute-start | bytes 589832 | tf_op jit(solution)/shard_map/ppermute | solution.py:233
  38.2 4.3 %all-to-all-done.1.refs_0_ = f32[16,32,128]{2,1,0:T(8,128)S(1)} async-done(((f32[16,32,128]{2,1,0:T(8,128)}), f32[16,32,128]{2,1,0:T(8,128)S(1)}, u32[]{:S(2)}, u32[]{:S(2)}) %all-to-all-start.1) | async-done | bytes 262176 | tf_op jit(solution)/shard_map/all_to_all | solution.py:245
  42.5 4.5 %collective-permute-done.3.s3 = bf16[16,6144]{1,0:T(8,128)(2,1)S(1)} collective-permute-done((bf16[16,6144]{1,0:T(8,128)(2,1)S(1)}, bf16[16,6144]{1,0:T(8,128)(2,1)S(1)}, u32[]{:S(2)}, u32[]{:S(2)}) %collective-permute-start.3) | collective-permute-done | bytes 196640 | tf_op jit(solution)/shard_map/ppermute | solution.py:233
  47.0 0.0 collective-permute-done.2.s2
  47.0 0.0 collective-permute-done.1.s1
  47.0 0.0 copy-done.2
  47.0 0.0 copy-start.1
  47.0 2.8 %copy-done.1 = f32[12552,128]{1,0:T(8,128)S(1)} copy-done((f32[12552,128]{1,0:T(8,128)S(1)}, f32[12552,128]{1,0:T(8,128)}, u32[]{:S(2)}) %copy-start.1) | copy-done | bytes 6426648
  49.8 5.3 %update.1 = (f32[80,80]{1,0:T(8,128)}, bf16[64,192,128]{2,1,0:T(8,128)(2,1)}, s32[1,1]{1,0:T(1,128)}) custom-call(f32[1,32,128]{2,1,0:T(8,128)S(1)} %combine.5.total_ref, f32[1,64]{1,0:T(1,128)S(1)} %bitcast.12, bf16[16,6144]{1,0:T(8,128)(2,1)S(1)} %snapshots.1.snap_ref.s0, bf16[16,6144]{1,0:T(8,128)(2,1)S(1)} %collective-permute-done.1.s1, ...), custom_call_target="tpu_custom_call" | custom-call | tf_op jit(solution)/shard_map/update/pallas_call | solution.py:212
  (2 shorter events, 0.0 us)
Async XLA Ops:
  1.3 2.0 %copy-start.3 = (bf16[64,3,4,2048]{3,2,1,0:T(4,128)(2,1)S(1)}, bf16[64,3,4,2048]{3,2,1,0:T(4,128)(2,1)}, u32[]{:S(2)}) copy-start(bf16[64,3,4,2048]{3,2,1,0:T(4,128)(2,1)} %param.5) | copy-start | bytes 9437188
  2.5 44.5 %copy-start.2 = (f32[64]{0:T(128)S(1)}, f32[64]{0:T(128)}, u32[]{:S(2)}) copy-start(f32[64]{0:T(128)} %param.6) | copy-start | bytes 772
  4.4 2.7 %copy-start = (f32[12552,128]{1,0:T(8,128)}, f32[12552,128]{1,0:T(8,128)S(1)}, u32[]{:S(2)}) copy-start(f32[12552,128]{1,0:T(8,128)S(1)} %get-tuple-element.11.wide_ref) | copy-start | bytes 19279876
  7.1 1.2 %collective-permute-start = (f32[1,32,128]{2,1,0:T(8,128)S(1)}, f32[1,32,128]{2,1,0:T(8,128)S(1)}, u32[]{:S(2)}, u32[]{:S(2)}) collective-permute-start(f32[1,32,128]{2,1,0:T(8,128)S(1)} %get-tuple-element.10.refs_0_), channel_id=1, source_target_pairs={{0,1},{1,0},{2,3},{3,2},{4,5},{5,4},{6,7},{7,6},{8,9},{9,8},{10,11... | collective-permute-start | bytes 49160 | tf_op jit(solution)/shard_map/ppermute | solution.py:242
  26.7 15.8 %all-to-all-start.1 = ((f32[16,32,128]{2,1,0:T(8,128)}), f32[16,32,128]{2,1,0:T(8,128)S(1)}, u32[]{:S(2)}, u32[]{:S(2)}) async-start(f32[16,32,128]{2,1,0:T(8,128)} %combine.4), calls=%async_computation.1 | async-start | bytes 524288 | tf_op jit(solution)/shard_map/all_to_all | solution.py:245
  34.1 12.8 %collective-permute-start.3 = (bf16[16,6144]{1,0:T(8,128)(2,1)S(1)}, bf16[16,6144]{1,0:T(8,128)(2,1)S(1)}, u32[]{:S(2)}, u32[]{:S(2)}) collective-permute-start(bf16[16,6144]{1,0:T(8,128)(2,1)S(1)} %snapshots.1.snap_ref.s0), channel_id=1, source_target_pairs={{0,192},{64,128},{128,64},{192,0},{1,193},{65,129},{129,65},{193,1... | collective-permute-start | bytes 589832 | tf_op jit(solution)/shard_map/ppermute | solution.py:233
  36.8 10.2 %collective-permute-start.2 = (bf16[16,6144]{1,0:T(8,128)(2,1)S(1)}, bf16[16,6144]{1,0:T(8,128)(2,1)S(1)}, u32[]{:S(2)}, u32[]{:S(2)}) collective-permute-start(bf16[16,6144]{1,0:T(8,128)(2,1)S(1)} %snapshots.1.snap_ref.s0), channel_id=1, source_target_pairs={{0,128},{64,192},{128,0},{192,64},{1,129},{65,193},{129,1},{193,65... | collective-permute-start | bytes 589832 | tf_op jit(solution)/shard_map/ppermute | solution.py:233
  37.7 9.3 %collective-permute-start.1 = (bf16[16,6144]{1,0:T(8,128)(2,1)S(1)}, bf16[16,6144]{1,0:T(8,128)(2,1)S(1)}, u32[]{:S(2)}, u32[]{:S(2)}) collective-permute-start(bf16[16,6144]{1,0:T(8,128)(2,1)S(1)} %snapshots.1.snap_ref.s0), channel_id=1, source_target_pairs={{0,64},{64,0},{128,192},{192,128},{1,65},{65,1},{129,193},{193,129... | collective-permute-start | bytes 589832 | tf_op jit(solution)/shard_map/ppermute | solution.py:233
  47.0 2.8 %copy-start.1 = (f32[12552,128]{1,0:T(8,128)S(1)}, f32[12552,128]{1,0:T(8,128)}, u32[]{:S(2)}) copy-start(f32[12552,128]{1,0:T(8,128)} %copy-done) | copy-start | bytes 19279876
